TPU v7x, 256 devices: a 8x8x2 block of a 8x8x16 slice. The times are simulated.
256 devices in a mesh: rep: 2 (over z), blk: 128 (over x, y, core).
Axes of the slice: x: 8, y: 8, z: 2, core: 2. Of those that a mesh axis runs over, the one named last changes fastest.
The devices are a block of a 8x8x16 slice.
Arguments:
- hidden: bfloat16 [32, 4096], P('rep', 'blk'), parts along dimension 0, may hold values from -4 to 4
- queries: bfloat16 [32, 4096], P('rep'), parts along dimension 0, may hold values from -180 to 180
- cache_kv: bfloat16 [2, 32, 4096, 1024], P(None, 'rep', 'blk'), parts along dimension 1, may hold values from -6 to 6
- cache_len: int32 [32], P('rep'), parts along dimension 0, may hold values from 1 to 4096
- inserted_key_value: bfloat16 [2, 16, 4096, 1024], P(None, 'rep', 'blk'), parts along dimension 1, may hold values from -6 to 6
- insert_slot: int32 [16], P('rep'), parts along dimension 0, may hold values from 0 to 15, as said below
- prefix_len: int32 [16], P('rep'), parts along dimension 0, may hold values from 1 to 4096, as said below
- out_weight: bfloat16 [4096, 4096], P(None, 'blk'), may hold values from -0.09375 to 0.09375
- norm_gain: bfloat16 [4096], replicated, may hold values from 0.25 to 1.75
- router_weight: bfloat16 [4096, 4], replicated, may hold values from -0.09375 to 0.09375
- expert_ids: int32 [32, 2], P('rep'), parts along dimension 0, may hold values from 0 to 3, all different within a row
- gate_up: bfloat16 [2, 4096, 28672], P(None, None, 'blk'), may hold values from -0.09375 to 0.09375
- down_proj: bfloat16 [28672, 4096], P('blk'), may hold values from -0.0625 to 0.0625
Outputs:
- layer_out: bfloat16 [32, 4096], P('rep', 'blk'), parts along dimension 0
There are 2 independent parts, one for each index of `rep`. A program takes and returns all parts, laid end to end along the dimension named above; an argument that names none is the same for every part. Nothing has to cross between parts.
Inputs may be any that keep to these rules, and one draw needn't show every extreme that they name: `insert_slot`: 8 different slot numbers. `prefix_len`: some inserted request has all 4096 positions.
All inputs are finite; a program needn't handle non-finite values.
Results may differ from a plain program's by a relative error of at most 0.012.
Values may be sent and summed in bfloat16 or wider, within the bound.
A program may use at most 128 MiB of HBM per device.

v0:
```python
import math
import jax
import jax.numpy as jnp
from jax import lax
from jax.sharding import Mesh
from jax.sharding import PartitionSpec as P

QUERY_HEADS = 32
KEY_VALUE_HEADS = 8
HEAD_SIZE = 128
EXPERTS = 4
FF = 7168
BLK = ("blk_0", "blk_1", "blk_2")


def shifted(shard, axis, by):
    count = lax.axis_size(axis)
    return lax.ppermute(shard, axis, [(i, (i + by) % count) for i in range(count)])


def all_in_one(shard, axis):
    leaves = jax.tree.leaves(shard)
    order = sorted(range(len(leaves)), key=lambda k: -leaves[k].size)
    width = (1, *leaves[order[0]].shape)[-1]
    lines = [
        jnp.pad(leaves[k].reshape(-1), (0, -leaves[k].size % width)).reshape(-1, width)
        for k in order
    ]
    both, at, found = (lax.all_gather(jnp.concatenate(lines), axis), 0, {})
    for k, line in zip(order, lines):
        piece = both[:, at : at + len(line)].reshape(len(both), -1)
        found[k] = piece[:, : leaves[k].size].reshape(-1, *leaves[k].shape)
        at += len(line)
    numbers = iter(range(len(leaves)))
    return jax.tree.map(lambda _: found[next(numbers)], shard)


def combined_by_axis(shard, axes, combine):
    for axis in axes:
        pieces = all_in_one(shard, axis)
        shard = jax.tree.map(lambda part: part[0], pieces)
        for k in range(1, lax.axis_size(axis)):
            shard = combine(shard, jax.tree.map(lambda part: part[k], pieces))
    return shard


def sum_in_order(tiles, axes, order):
    inside = tiles.shape[1:]
    tiles = tiles.reshape(*(lax.axis_size(a) for a in axes), *inside)
    tiles = jnp.moveaxis(tiles, order, range(len(axes))).reshape(-1, *inside)
    for k in order:
        tiles = lax.psum_scatter(tiles, axes[k], scatter_dimension=0, tiled=True)
    return tiles[0]


def split_up(shard, dim, count):
    before, after = (shard.shape[:dim], shard.shape[dim + 1 :])
    return jnp.moveaxis(shard.reshape(*before, count, -1, *after), dim, 0)


def summed_rows(shard, axes, order, dim):
    count = lax.axis_size(axes)
    return sum_in_order(split_up(shard, dim, count), axes, order)


def block_attention(queries, key_rows, value_rows, valid):
    slot_list = queries.shape[0]
    query_groups = QUERY_HEADS // KEY_VALUE_HEADS
    heads_of_queries = queries.astype(jnp.float32).reshape(
        slot_list, KEY_VALUE_HEADS, query_groups, HEAD_SIZE
    )
    heads_of_keys = key_rows.astype(jnp.float32).reshape(slot_list, -1, KEY_VALUE_HEADS, HEAD_SIZE)
    heads_of_values = value_rows.astype(jnp.float32).reshape(
        slot_list, -1, KEY_VALUE_HEADS, HEAD_SIZE
    )
    scores = jnp.einsum("skgd,sckd->skgc", heads_of_queries, heads_of_keys) / math.sqrt(HEAD_SIZE)
    masked = valid[:, None, None, :]
    peak = jnp.max(jnp.where(masked, scores, -1e30), axis=-1)
    weights = jnp.where(masked, jnp.exp(scores - peak[..., None]), 0.0)
    totals = jnp.sum(weights, axis=-1)
    partial_value = jnp.einsum("skgc,sckd->skgd", weights, heads_of_values)
    return (
        partial_value.reshape(slot_list, QUERY_HEADS, HEAD_SIZE),
        peak.reshape(slot_list, QUERY_HEADS),
        totals.reshape(slot_list, QUERY_HEADS),
    )


def merge_pair(earlier, later):
    early_out, early_peak, early_total = earlier
    late_out, late_peak, late_total = later
    highest = jnp.maximum(early_peak, late_peak)
    early_scale = jnp.exp(early_peak - highest)
    late_scale = jnp.exp(late_peak - highest)
    merged_out = early_out * early_scale[..., None] + late_out * late_scale[..., None]
    return (merged_out, highest, early_total * early_scale + late_total * late_scale)


def route_shares(normed, router_weight, expert_ids):
    logits = jnp.dot(normed, router_weight, preferred_element_type=jnp.float32)
    chosen = (expert_ids[:, :, None] == jnp.arange(EXPERTS, dtype=jnp.int32)[None, None, :]).astype(
        jnp.float32
    )
    picked = jnp.sum(chosen * logits[:, None, :], axis=-1)
    gates = jax.nn.sigmoid(picked - picked[:, ::-1])
    return jnp.sum(gates[:, :, None] * chosen, axis=1)


def on_device(
    hidden,
    queries,
    cache_kv,
    cache_len,
    inserted_key_value,
    insert_slot,
    prefix_len,
    out_weight,
    norm_gain,
    router_weight,
    expert_ids,
    gate_up,
    down_proj,
):
    cycle_size = lax.axis_size(BLK)
    dev_index = lax.axis_index(BLK)
    half_cycle = cycle_size // 2
    ctx_rows = cache_kv.shape[2]
    arrived = shifted(inserted_key_value, BLK, half_cycle)
    cache = cache_kv.at[:, insert_slot].set(arrived)
    slot_lengths = cache_len.at[insert_slot].set(prefix_len)
    positions = dev_index * ctx_rows + jnp.arange(ctx_rows, dtype=jnp.int32)
    valid = positions[None, :] < slot_lengths[:, None]
    partial_value, peak, totals = block_attention(queries, cache[0], cache[1], valid)
    slot_list = queries.shape[0]
    summed, highest, all_totals = combined_by_axis((partial_value, peak, totals), BLK, merge_pair)
    attn = (
        (summed / all_totals[..., None])
        .reshape(slot_list, QUERY_HEADS * HEAD_SIZE)
        .astype(jnp.bfloat16)
    )
    local_mixed = (
        hidden.astype(jnp.float32) + jnp.dot(attn, out_weight, preferred_element_type=jnp.float32)
    ).astype(jnp.bfloat16)
    mixed = lax.all_gather(local_mixed, BLK, axis=1, tiled=True)
    mixed_f = mixed.astype(jnp.float32)
    scale = lax.rsqrt(jnp.mean(mixed_f * mixed_f, axis=-1, keepdims=True) + 1e-05)
    normed = (mixed_f * scale * norm_gain.astype(jnp.float32)).astype(jnp.bfloat16)
    shares = route_shares(normed, router_weight, expert_ids)
    unit_count = gate_up.shape[2]
    expert_now = dev_index * unit_count // FF
    picker = (jnp.arange(EXPERTS, dtype=jnp.int32) == expert_now).astype(jnp.float32)
    expert_share = jnp.sum(shares * picker[None, :], axis=1)
    act = (
        jax.nn.silu(jnp.dot(normed, gate_up[0], preferred_element_type=jnp.float32))
        * jnp.dot(normed, gate_up[1], preferred_element_type=jnp.float32)
    ).astype(jnp.bfloat16)
    term = expert_share[:, None] * jnp.dot(act, down_proj, preferred_element_type=jnp.float32)
    moe = summed_rows(term, BLK, (2, 0, 1), 1)
    return (local_mixed.astype(jnp.float32) + moe).astype(jnp.bfloat16)


def solution(mesh):
    split = Mesh(
        mesh.devices.reshape(mesh.shape["rep"], 8, 8, 2), ("rep", "blk_0", "blk_1", "blk_2")
    )
    return jax.shard_map(
        on_device,
        mesh=split,
        in_specs=(
            P("rep", BLK),
            P("rep", None),
            P(None, "rep", BLK, None),
            P("rep"),
            P(None, "rep", BLK, None),
            P("rep"),
            P("rep"),
            P(None, BLK),
            P(),
            P(),
            P("rep", None),
            P(None, None, BLK),
            P(BLK, None),
        ),
        out_specs=P("rep", BLK),
        check_vma=False,
    )
```

profile of v0, /device:TPU:514, one launch (start us, length us, event | category | flops | bytes accessed | tf_op | source)
XLA Modules:
  0.0 353.1 jit_solution(5497632940912069190)
XLA Ops:
  6.6 3.3 copy.67
  9.9 5.1 %collective-permute-start = (bf16[2,8,32,1024]{3,2,1,0:T(8,128)(2,1)}, bf16[2,8,32,1024]{3,2,1,0:T(8,128)(2,1)S(1)}, u32[]{:S(2)}, u32[]{:S(2)}) collective-permute-start(bf16[2,8,32,1024]{3,2,1,0:T(8,128)(2,1)} %param.17), channel_id=1, source_target_pairs={{0,64},{1,65},{2,66},{3,67},{4,68},{5,69},{6,70},{7,71},{8,72},{9,... | collective-permute-start | bytes 3145736 | tf_op jit(solution)/shard_map/ppermute | solution.py:18
  15.2 0.6 scatter_fusion
  15.9 44.1 %collective-permute-done = bf16[2,8,32,1024]{3,2,1,0:T(8,128)(2,1)S(1)} collective-permute-done((bf16[2,8,32,1024]{3,2,1,0:T(8,128)(2,1)}, bf16[2,8,32,1024]{3,2,1,0:T(8,128)(2,1)S(1)}, u32[]{:S(2)}, u32[]{:S(2)}) %collective-permute-start) | collective-permute-done | bytes 1048608 | tf_op jit(solution)/shard_map/ppermute | solution.py:18
  60.0 1.0 copy-done.2
  60.9 1.3 copy.39
  62.3 2.9 scatter_fusion.1
  65.1 1.7 fusion.176
  66.9 0.3 copy.46
  67.1 0.3 copy.47
  67.4 0.7 select_reduce_fusion
  68.3 0.4 fusion.62
  68.7 0.4 fusion.15
  69.2 0.7 pad_maximum_fusion
  70.1 61.1 %all-gather.7.cloned.1.call-done = f32[4160,128]{1,0:T(8,128)} async-done(((f32[520,128]{1,0:T(8,128)}), f32[4160,128]{1,0:T(8,128)}) %all-gather.7.cloned.1.call-update) | async-done | bytes 2129936 | tf_op jit(solution)/shard_map/all_gather | solution.py:29
  131.2 0.7 fusion.151
  131.9 0.8 fusion.102
  132.7 0.7 fusion.150
  133.4 0.7 fusion.148
  134.1 0.7 fusion.146
  134.8 2.5 fusion.42
  137.3 0.7 pad_maximum_fusion.1
  138.2 41.5 %all-gather.9.cloned.1.call-done = f32[4160,128]{1,0:T(8,128)} async-done(((f32[520,128]{1,0:T(8,128)}), f32[4160,128]{1,0:T(8,128)}) %all-gather.9.cloned.1.call-update) | async-done | bytes 2129936 | tf_op jit(solution)/shard_map/all_gather | solution.py:29
  179.7 0.7 fusion.136
  180.4 0.8 fusion.81
  181.2 0.7 fusion.135
  181.9 0.7 fusion.133
  182.6 0.7 fusion.131
  183.3 2.5 fusion.21
  185.9 2.4 all-gather.2
  188.9 0.1 mul.560
  189.0 0.1 div.33
  189.1 0.6 fusion.14
  189.8 50.2 %all-gather.3 = bf16[128,32,16]{1,2,0:T(8,128)(2,1)S(1)} all-gather(bf16[1,32,16]{1,2,0:T(8,128)(2,1)S(1)} %bitcast.762), channel_id=1, replica_groups=mesh['rep'=2,'blk_0'=8,'blk_1'=8,'blk_2'=2] {'blk_0','blk_1','blk_2'}, dimensions={0}, use_global_device_ids=true | all-gather | bytes 132096 | tf_op jit(solution)/shard_map/all_gather | solution.py:144
  239.9 0.5 copy.42
  240.5 0.2 copy.43
  240.7 0.5 reshape.962
  241.2 0.1 multiply_reduce_fusion
  241.5 2.1 fusion.2
  243.6 0.2 fusion.179
  243.9 2.9 convolution_multiply_fusion
  246.8 0.3 reshape.936
  247.2 0.6 copy.44
  247.8 1.1 copy.45
  249.0 14.1 %reduce-scatter.4.cloned.1.call-done = f32[64,16,32]{2,1,0:T(8,128)} async-done(((f32[128,16,32]{2,1,0:T(8,128)}), f32[64,16,32]{2,1,0:T(8,128)}) %reduce-scatter.4.cloned.1.call-update) | async-done | bytes 131088 | tf_op jit(solution)/shard_map/reduce_scatter | solution.py:52
  263.3 41.8 %reduce-scatter.6.cloned.1.call-done = f32[8,16,32]{2,1,0:T(8,128)} async-done(((f32[64,16,32]{2,1,0:T(8,128)}), f32[8,16,32]{2,1,0:T(8,128)}) %reduce-scatter.6.cloned.1.call-update) | async-done | bytes 16400 | tf_op jit(solution)/shard_map/reduce_scatter | solution.py:52
  305.1 40.1 %reduce-scatter.8.cloned.1.call-done = f32[1,16,32]{2,1,0:T(8,128)} async-done(((f32[8,16,32]{2,1,0:T(8,128)}), f32[1,16,32]{2,1,0:T(8,128)}) %reduce-scatter.8.cloned.1.call-update) | async-done | bytes 2064 | tf_op jit(solution)/shard_map/reduce_scatter | solution.py:52
  345.3 1.3 fusion.74
  (57 shorter events, 1.9 us)
Async XLA Ops:
  6.5 237.4 %copy-start = (bf16[224,4096]{1,0:T(8,128)(2,1)S(1)}, bf16[224,4096]{1,0:T(8,128)(2,1)}, u32[]{:S(2)}) copy-start(bf16[224,4096]{1,0:T(8,128)(2,1)} %param.25) | copy-start | bytes 5505028
  6.6 8.5 %copy-start.4 = (bf16[16,4096]{1,0:T(8,128)(2,1)S(1)}, bf16[16,4096]{1,0:T(8,128)(2,1)}, u32[]{:S(2)}) copy-start(bf16[16,4096]{1,0:T(8,128)(2,1)} %param.14) | copy-start | bytes 393220
  6.6 124.6 %all-gather.7.cloned.1.call-start = ((), (), s32[]{:S(2)}) async-start(), calls=%async_computation.6 | async-start | bytes 2396160 | tf_op jit(solution)/shard_map/all_gather | solution.py:29
  6.6 8.6 %copy-start.10 = (s32[8]{0:T(128)S(1)}, s32[8]{0:T(128)}, u32[]{:S(2)}) copy-start(s32[8]{0:T(128)} %param.18) | copy-start | bytes 100
  6.6 8.6 %copy-start.1 = (s32[16]{0:T(128)S(1)}, s32[16]{0:T(128)}, u32[]{:S(2)}) copy-start(s32[16]{0:T(128)} %param.16) | copy-start | bytes 196
  6.6 8.6 %copy-start.8 = (s32[8]{0:T(128)S(1)}, s32[8]{0:T(128)}, u32[]{:S(2)}) copy-start(s32[8]{0:T(128)} %param.19) | copy-start | bytes 100
  9.9 50.0 %collective-permute-start = (bf16[2,8,32,1024]{3,2,1,0:T(8,128)(2,1)}, bf16[2,8,32,1024]{3,2,1,0:T(8,128)(2,1)S(1)}, u32[]{:S(2)}, u32[]{:S(2)}) collective-permute-start(bf16[2,8,32,1024]{3,2,1,0:T(8,128)(2,1)} %param.17), channel_id=1, source_target_pairs={{0,64},{1,65},{2,66},{3,67},{4,68},{5,69},{6,70},{7,71},{8,72},{9,... | collective-permute-start | bytes 3145736 | tf_op jit(solution)/shard_map/ppermute | solution.py:18
  59.9 1.0 copy-start.2
  69.1 69.0 %copy-start.5 = (bf16[4096]{0:T(1024)(128)(2,1)S(1)}, bf16[4096]{0:T(1024)(128)(2,1)}, u32[]{:S(2)}) copy-start(bf16[4096]{0:T(1024)(128)(2,1)} %param.21) | copy-start | bytes 24580
  70.0 109.7 %all-gather.9.cloned.1.call-start = ((), (), s32[]{:S(2)}) async-start(), calls=%async_computation.7 | async-start | bytes 2396160 | tf_op jit(solution)/shard_map/all_gather | solution.py:29
  138.1 125.1 %reduce-scatter.4.cloned.1.call-start = ((), (), s32[]{:S(2)}) async-start(), calls=%async_computation.3 | async-start | bytes 1572864 | tf_op jit(solution)/shard_map/reduce_scatter | solution.py:52
  185.8 3.3 copy-start.3
  185.8 3.3 copy-start.6
  240.7 2.9 copy-start.9
  240.7 3.0 copy-start.7
  248.9 56.1 %reduce-scatter.6.cloned.1.call-start = ((), (), s32[]{:S(2)}) async-start(), calls=%async_computation.4 | async-start | bytes 589824 | tf_op jit(solution)/shard_map/reduce_scatter | solution.py:52
  263.2 82.1 %reduce-scatter.8.cloned.1.call-start = ((), (), s32[]{:S(2)}) async-start(), calls=%async_computation.5 | async-start | bytes 73728 | tf_op jit(solution)/shard_map/reduce_scatter | solution.py:52
Sparse Core Ops, SparseCore 0:
  70.1 61.0 all-gather.6
  138.2 41.4 all-gather.8
  249.1 14.0 reduce-scatter.3
  265.5 39.5 reduce-scatter.5
  307.4 37.7 reduce-scatter.7
where the time goes:
time: 354 us; the launch traced here: 353 us
  waiting for transfers between devices  243 us (69%)
  blocking collectives  52.5 us (15%)
  local copies, waits for them, and re-layouts  15.9 us (4%)
  other arithmetic  15.8 us (4%)
  between operations  13.6 us (4%)
  matrix products  6.93 us (2%)
  starting transfers between devices  5.39 us (2%)
    all_gather x2, waiting for transfers between devices, all_in_one(): both, at, found = (lax.all_gather(jnp.concatenate(lines), axis), 0, {})  103 us
    reduce_scatter x3, waiting for transfers between devices, sum_in_order(): tiles = lax.psum_scatter(tiles, axes[k], scatter_dimension=0, tiled=True)  96.1 us
    all_gather x1, blocking collectives, on_device(): mixed = lax.all_gather(local_mixed, BLK, axis=1, tiled=True)  50.2 us
    ppermute x1, waiting for transfers between devices, shifted(): lax.ppermute(shard, axis, [(i, (i + by) % count) for i in range(count)])  44.1 us
  transfers between devices with their start and end apart: 6, of which 6 were waited for; matrix products, arithmetic and copies ran while one was open for 0% of the time, Pallas kernels for 0%

commit v1 on v0

--- a/solution.py
+++ b/solution.py
@@ -141,7 +141,9 @@
     local_mixed = (
         hidden.astype(jnp.float32) + jnp.dot(attn, out_weight, preferred_element_type=jnp.float32)
     ).astype(jnp.bfloat16)
-    mixed = lax.all_gather(local_mixed, BLK, axis=1, tiled=True)
+    mixed = jnp.concatenate(
+        lax.all_to_all(jnp.stack([local_mixed] * lax.axis_size(BLK)), BLK, 0, 0), axis=1
+    )
     mixed_f = mixed.astype(jnp.float32)
     scale = lax.rsqrt(jnp.mean(mixed_f * mixed_f, axis=-1, keepdims=True) + 1e-05)
     normed = (mixed_f * scale * norm_gain.astype(jnp.float32)).astype(jnp.bfloat16)

time: 354 us -> 327 us (0.924)
  blocking collectives: 52.5 us -> 2.37 us
  starting transfers between devices: 5.39 us -> 18.5 us
  waiting for transfers between devices: 243 us -> 249 us
    all_gather x1 -> x0, blocking collectives: 50.2 us -> none  [on_device(): mixed = lax.all_gather(local_mixed, BLK, axis=1, tiled=True)]
    all_to_all x0 -> x1, starting transfers between devices: none -> 13 us  [on_device(): lax.all_to_all(jnp.stack([local_mixed] * lax.axis_size(BLK)), BLK, 0, 0)]
    all_to_all x0 -> x1, waiting for transfers between devices: none -> 11 us  [on_device(): lax.all_to_all(jnp.stack([local_mixed] * lax.axis_size(BLK)), BLK, 0, 0)]
    reduce_scatter x3, waiting for transfers between devices: 96.1 us -> 91.3 us  [sum_in_order(): tiles = lax.psum_scatter(tiles, axes[k], scatter_dimension=0, tiled=True)]
  transfers between devices with their start and end apart: 6 -> 7, of which waited for: 6 -> 7; matrix products, arithmetic and copies ran while one was open for 0% -> 0% of each run, Pallas kernels for 0% -> 0%
where the time goes in v1:
time: 327 us; the launch traced here: 326 us
  waiting for transfers between devices  249 us (76%)
  starting transfers between devices  18.5 us (6%)
  local copies, waits for them, and re-layouts  18.3 us (6%)
  other arithmetic  16.2 us (5%)
  between operations  13.6 us (4%)
  matrix products  7.95 us (2%)
    all_gather x2, waiting for transfers between devices, all_in_one(): both, at, found = (lax.all_gather(jnp.concatenate(lines), axis), 0, {})  103 us
    reduce_scatter x3, waiting for transfers between devices, sum_in_order(): tiles = lax.psum_scatter(tiles, axes[k], scatter_dimension=0, tiled=True)  91.3 us
    ppermute x1, waiting for transfers between devices, shifted(): lax.ppermute(shard, axis, [(i, (i + by) % count) for i in range(count)])  44.1 us
    all_to_all x1, starting transfers between devices, on_device(): lax.all_to_all(jnp.stack([local_mixed] * lax.axis_size(BLK)), BLK, 0, 0)  13 us
    all_to_all x1, waiting for transfers between devices, on_device(): lax.all_to_all(jnp.stack([local_mixed] * lax.axis_size(BLK)), BLK, 0, 0)  11 us
  transfers between devices with their start and end apart: 7, of which 7 were waited for; matrix products, arithmetic and copies ran while one was open for 0% of the time, Pallas kernels for 0%

profile of v1, /device:TPU:514, one launch (start us, length us, event | category | flops | bytes accessed | tf_op | source)
XLA Modules:
  0.0 326.2 jit_solution(1636406483602804444)
XLA Ops:
  6.6 3.3 %copy.61 = bf16[2,16,32,1024]{3,2,1,0:T(8,128)(2,1)} copy(bf16[2,16,32,1024]{3,2,1,0:T(8,128)(2,1)} %param.15) | data formatting | bytes 4194304
  9.9 5.1 %collective-permute-start = (bf16[2,8,32,1024]{3,2,1,0:T(8,128)(2,1)}, bf16[2,8,32,1024]{3,2,1,0:T(8,128)(2,1)S(1)}, u32[]{:S(2)}, u32[]{:S(2)}) collective-permute-start(bf16[2,8,32,1024]{3,2,1,0:T(8,128)(2,1)} %param.17), channel_id=1, source_target_pairs={{0,64},{1,65},{2,66},{3,67},{4,68},{5,69},{6,70},{7,71},{8,72},{9,... | collective-permute-start | bytes 3145736 | tf_op jit(solution)/shard_map/ppermute | solution.py:18
  15.2 0.6 scatter_fusion
  15.9 44.1 %collective-permute-done = bf16[2,8,32,1024]{3,2,1,0:T(8,128)(2,1)S(1)} collective-permute-done((bf16[2,8,32,1024]{3,2,1,0:T(8,128)(2,1)}, bf16[2,8,32,1024]{3,2,1,0:T(8,128)(2,1)S(1)}, u32[]{:S(2)}, u32[]{:S(2)}) %collective-permute-start) | collective-permute-done | bytes 1048608 | tf_op jit(solution)/shard_map/ppermute | solution.py:18
  59.9 1.0 copy-done.2
  60.9 1.3 copy.33
  62.2 2.9 scatter_fusion.1
  65.1 1.7 fusion.183
  67.1 0.3 copy.41
  67.4 0.7 select_reduce_fusion
  68.3 0.4 fusion.66
  68.7 0.4 fusion.18
  69.2 0.7 pad_maximum_fusion
  70.1 61.1 %all-gather.6.cloned.1.call-done = f32[4160,128]{1,0:T(8,128)} async-done(((f32[520,128]{1,0:T(8,128)}), f32[4160,128]{1,0:T(8,128)}) %all-gather.6.cloned.1.call-update) | async-done | bytes 2129936 | tf_op jit(solution)/shard_map/all_gather | solution.py:29
  131.2 0.7 fusion.158
  131.8 0.8 fusion.109
  132.7 0.7 fusion.157
  133.4 0.7 fusion.155
  134.1 0.7 fusion.153
  134.8 2.5 fusion.46
  137.3 0.7 pad_maximum_fusion.1
  138.1 41.6 %all-gather.8.cloned.1.call-done = f32[4160,128]{1,0:T(8,128)} async-done(((f32[520,128]{1,0:T(8,128)}), f32[4160,128]{1,0:T(8,128)}) %all-gather.8.cloned.1.call-update) | async-done | bytes 2129936 | tf_op jit(solution)/shard_map/all_gather | solution.py:29
  179.7 0.7 fusion.143
  180.4 0.8 fusion.88
  181.2 0.7 fusion.142
  181.9 0.7 fusion.140
  182.6 0.7 fusion.138
  183.3 2.5 fusion.25
  185.9 2.4 all-gather.2
  189.2 0.6 fusion.14
  189.9 1.0 reshape.987
  190.9 13.0 %all-to-all-start = ((bf16[128,2,256]{2,1,0:T(2,128)(2,1)}), bf16[128,2,256]{2,1,0:T(2,128)(2,1)S(1)}, u32[]{:S(2)}, u32[]{:S(2)}) async-start(bf16[128,2,256]{2,1,0:T(2,128)(2,1)} %reshape.987), calls=%async_computation | async-start | bytes 262144 | tf_op jit(solution)/shard_map/all_to_all | solution.py:145
  204.2 11.0 %all-to-all-done = bf16[128,2,256]{2,1,0:T(2,128)(2,1)S(1)} async-done(((bf16[128,2,256]{2,1,0:T(2,128)(2,1)}), bf16[128,2,256]{2,1,0:T(2,128)(2,1)S(1)}, u32[]{:S(2)}, u32[]{:S(2)}) %all-to-all-start) | async-done | bytes 131104 | tf_op jit(solution)/shard_map/all_to_all | solution.py:145
  215.2 0.3 reshape.988
  215.6 0.3 fusion.15
  215.9 0.3 copy.36
  216.2 1.2 reshape.965
  217.4 1.2 fusion.67
  219.1 0.5 convert_element_type.65
  219.7 2.1 fusion.2
  221.8 2.9 convolution_multiply_fusion
  224.7 0.3 reshape.962
  225.0 0.6 copy.38
  225.6 1.1 copy.39
  226.9 9.2 %reduce-scatter.4.cloned.1.call-done = f32[64,16,32]{2,1,0:T(8,128)} async-done(((f32[128,16,32]{2,1,0:T(8,128)}), f32[64,16,32]{2,1,0:T(8,128)}) %reduce-scatter.4.cloned.1.call-update) | async-done | bytes 131088 | tf_op jit(solution)/shard_map/reduce_scatter | solution.py:52
  236.2 41.8 %reduce-scatter.6.cloned.1.call-done = f32[8,16,32]{2,1,0:T(8,128)} async-done(((f32[64,16,32]{2,1,0:T(8,128)}), f32[8,16,32]{2,1,0:T(8,128)}) %reduce-scatter.6.cloned.1.call-update) | async-done | bytes 16400 | tf_op jit(solution)/shard_map/reduce_scatter | solution.py:52
  278.1 40.2 %reduce-scatter.8.cloned.1.call-done = f32[1,16,32]{2,1,0:T(8,128)} async-done(((f32[8,16,32]{2,1,0:T(8,128)}), f32[1,16,32]{2,1,0:T(8,128)}) %reduce-scatter.8.cloned.1.call-update) | async-done | bytes 2064 | tf_op jit(solution)/shard_map/reduce_scatter | solution.py:52
  318.4 1.3 fusion.81
  (64 shorter events, 3.0 us)
Async XLA Ops:
  6.5 215.2 %copy-start = (bf16[224,4096]{1,0:T(8,128)(2,1)S(1)}, bf16[224,4096]{1,0:T(8,128)(2,1)}, u32[]{:S(2)}) copy-start(bf16[224,4096]{1,0:T(8,128)(2,1)} %param.25) | copy-start | bytes 5505028
  6.6 8.5 %copy-start.4 = (bf16[16,4096]{1,0:T(8,128)(2,1)S(1)}, bf16[16,4096]{1,0:T(8,128)(2,1)}, u32[]{:S(2)}) copy-start(bf16[16,4096]{1,0:T(8,128)(2,1)} %param.14) | copy-start | bytes 393220
  6.6 124.6 %all-gather.6.cloned.1.call-start = ((), (), s32[]{:S(2)}) async-start(), calls=%async_computation.7 | async-start | bytes 2396160 | tf_op jit(solution)/shard_map/all_gather | solution.py:29
  6.6 8.6 %copy-start.10 = (s32[8]{0:T(128)S(1)}, s32[8]{0:T(128)}, u32[]{:S(2)}) copy-start(s32[8]{0:T(128)} %param.18) | copy-start | bytes 100
  6.6 8.6 %copy-start.1 = (s32[16]{0:T(128)S(1)}, s32[16]{0:T(128)}, u32[]{:S(2)}) copy-start(s32[16]{0:T(128)} %param.16) | copy-start | bytes 196
  6.6 8.6 %copy-start.9 = (s32[8]{0:T(128)S(1)}, s32[8]{0:T(128)}, u32[]{:S(2)}) copy-start(s32[8]{0:T(128)} %param.19) | copy-start | bytes 100
  9.9 50.0 %collective-permute-start = (bf16[2,8,32,1024]{3,2,1,0:T(8,128)(2,1)}, bf16[2,8,32,1024]{3,2,1,0:T(8,128)(2,1)S(1)}, u32[]{:S(2)}, u32[]{:S(2)}) collective-permute-start(bf16[2,8,32,1024]{3,2,1,0:T(8,128)(2,1)} %param.17), channel_id=1, source_target_pairs={{0,64},{1,65},{2,66},{3,67},{4,68},{5,69},{6,70},{7,71},{8,72},{9,... | collective-permute-start | bytes 3145736 | tf_op jit(solution)/shard_map/ppermute | solution.py:18
  59.9 1.0 copy-start.2
  70.0 109.7 %all-gather.8.cloned.1.call-start = ((), (), s32[]{:S(2)}) async-start(), calls=%async_computation.8 | async-start | bytes 2396160 | tf_op jit(solution)/shard_map/all_gather | solution.py:29
  185.8 3.3 %copy-start.3 = (bf16[4096,32]{0,1:T(8,128)(2,1)S(1)}, bf16[4096,32]{0,1:T(8,128)(2,1)}, u32[]{:S(2)}) copy-start(bf16[4096,32]{0,1:T(8,128)(2,1)} %param.20) | copy-start | bytes 786436
  185.8 3.3 %copy-start.7 = (bf16[16,32]{1,0:T(8,128)(2,1)S(1)}, bf16[16,32]{1,0:T(8,128)(2,1)}, u32[]{:S(2)}) copy-start(bf16[16,32]{1,0:T(8,128)(2,1)} %param.13) | copy-start | bytes 3076
  188.3 15.8 %copy-start.6 = (bf16[4096]{0:T(1024)(128)(2,1)S(1)}, bf16[4096]{0:T(1024)(128)(2,1)}, u32[]{:S(2)}) copy-start(bf16[4096]{0:T(1024)(128)(2,1)} %param.21) | copy-start | bytes 24580
  190.9 24.3 %all-to-all-start = ((bf16[128,2,256]{2,1,0:T(2,128)(2,1)}), bf16[128,2,256]{2,1,0:T(2,128)(2,1)S(1)}, u32[]{:S(2)}, u32[]{:S(2)}) async-start(bf16[128,2,256]{2,1,0:T(2,128)(2,1)} %reshape.987), calls=%async_computation | async-start | bytes 262144 | tf_op jit(solution)/shard_map/all_to_all | solution.py:145
  203.9 32.2 %reduce-scatter.4.cloned.1.call-start = ((), (), s32[]{:S(2)}) async-start(), calls=%async_computation.4 | async-start | bytes 1572864 | tf_op jit(solution)/shard_map/reduce_scatter | solution.py:52
  215.6 1.9 copy-start.5
  215.6 3.0 copy-start.8
  226.8 51.3 %reduce-scatter.6.cloned.1.call-start = ((), (), s32[]{:S(2)}) async-start(), calls=%async_computation.5 | async-start | bytes 589824 | tf_op jit(solution)/shard_map/reduce_scatter | solution.py:52
  236.2 82.2 %reduce-scatter.8.cloned.1.call-start = ((), (), s32[]{:S(2)}) async-start(), calls=%async_computation.6 | async-start | bytes 73728 | tf_op jit(solution)/shard_map/reduce_scatter | solution.py:52
Sparse Core Ops, SparseCore 0:
  70.1 60.9 all-gather.5
  138.2 41.4 all-gather.7
  226.9 9.1 reduce-scatter.3
  238.5 39.5 reduce-scatter.5
  280.4 37.9 reduce-scatter.7
